TPU v7x, 32 devices: a whole 2x2x4 slice. The times are simulated.
32 devices in a mesh: row: 4 (over y, core), col: 8 (over z, x).
Axes of the slice: x: 2, y: 2, z: 4, core: 2. Of those that a mesh axis runs over, the one named last changes fastest.
Arguments:
- matrix: float32 [4096, 4096], P('row', 'col'), may hold values from -12 to 12, as said below
Outputs:
- sign_estimate: float32 [4096, 4096], P('row', 'col')
Inputs may be any that keep to these rules, and one draw needn't show every extreme that they name: `matrix`: symmetric; the magnitudes of its eigenvalues, divided by the root mean square of all its eigenvalues, lie between 0.4 and 1.7.
All inputs are finite; a program needn't handle non-finite values.
Results may differ from a plain program's by a relative error of at most 0.0002.
Values sent between devices are 32-bit elements; how exact they have to be, the bound alone decides.
A program may use at most 64 MiB of HBM per device.

v0:
```python
import jax
import jax.numpy as jnp
from jax import lax
from jax.sharding import PartitionSpec as P

N = 4096
ITERS = 2


def shards(matrix):
    total = lax.psum(jnp.sum(matrix * matrix), ("row", "col"))
    factor = jnp.sqrt(N / total)
    x_iter = matrix * factor
    for step in range(ITERS):
        source = x_iter
        rows_panel = lax.all_gather(source, "col", axis=1, tiled=True)
        cols_panel = lax.all_gather(source, "row", axis=0, tiled=True)
        square = jnp.dot(
            rows_panel,
            cols_panel,
            preferred_element_type=jnp.float32,
            precision=lax.Precision.HIGHEST,
        )
        cube_block = jnp.dot(
            rows_panel,
            lax.all_gather(square, "row", axis=0, tiled=True),
            preferred_element_type=jnp.float32,
            precision=lax.Precision.HIGHEST,
        )
        x_iter = 1.5 * x_iter - 0.5 * cube_block
    return x_iter


def solution(mesh):
    in_specs = (P("row", "col"),)
    out_specs = P("row", "col")
    return jax.shard_map(shards, mesh=mesh, in_specs=in_specs, out_specs=out_specs, check_vma=False)
```

profile of v0, /device:TPU:0, one launch (start us, length us, event | category | flops | bytes accessed | tf_op | source)
XLA Modules:
  0.0 875.6 jit_solution(11313682879477920894)
XLA Ops:
  6.5 0.0 all-gather.9.cloned.1.call-start
  6.5 2.7 multiply_reduce_fusion
  9.3 42.2 %psum.7 = f32[]{:T(128)} all-reduce(f32[]{:T(128)} %multiply_reduce_fusion), channel_id=1, replica_groups=mesh['row'=4,'col'=8] {'row','col'}, use_global_device_ids=true, to_apply=%region_1.0 | all-reduce | flops 1 | bytes 8 | tf_op jit(solution)/shard_map/psum | solution.py:11
  52.2 3.1 broadcast_multiply_fusion
  55.3 0.0 all-gather.9.cloned.1.call-update
  55.3 0.0 all-gather.7.cloned.1.call-start
  55.4 0.7 all-gather.7.cloned.1.call-update
  56.1 0.0 copy-start
  56.1 0.0 all-gather.11.cloned.1.call-start
  56.1 57.6 %all-gather.9.cloned.1.call-done = f32[4096,512]{1,0:T(8,128)} async-done(((f32[1024,512]{1,0:T(8,128)}), f32[4096,512]{1,0:T(8,128)}) %all-gather.9.cloned.1.call-update) | async-done | bytes 8388624 | tf_op jit(solution)/shard_map/all_gather | solution.py:17
  113.7 229.5 %all-gather.7.cloned.1.call-done = f32[1024,4096]{1,0:T(8,128)} async-done(((f32[1024,512]{1,0:T(8,128)}), f32[1024,4096]{1,0:T(8,128)}) %all-gather.7.cloned.1.call-update) | async-done | bytes 16777232 | tf_op jit(solution)/shard_map/all_gather | solution.py:16
  343.2 31.0 %fusion = f32[1024,512]{1,0:T(8,128)} fusion(f32[1024,4096]{1,0:T(8,128)} %all-gather.7.cloned.1.call-done, f32[4096,512]{1,0:T(8,128)} %all-gather.9.cloned.1.call-done), kind=kOutput, calls=%fused_computation.4 | convolution fusion | flops 25769803776 | bytes 27262976 | tf_op jit(solution)/shard_map/dot_general | solution.py:18
  374.2 0.0 all-gather.11.cloned.1.call-update
  374.2 0.2 all-gather.15.cloned.1.call-start
  374.5 56.4 %all-gather.11.cloned.1.call-done = f32[4096,512]{1,0:T(8,128)} async-done(((f32[1024,512]{1,0:T(8,128)}), f32[4096,512]{1,0:T(8,128)}) %all-gather.11.cloned.1.call-update) | async-done | bytes 8388624 | tf_op jit(solution)/shard_map/all_gather | solution.py:26
  430.8 0.0 copy-done
  430.8 31.2 %multiply_subtract_fusion.1 = f32[1024,512]{1,0:T(8,128)} fusion(f32[1024,512]{1,0:T(8,128)S(1)} %copy-done, f32[1024,4096]{1,0:T(8,128)} %all-gather.7.cloned.1.call-done, f32[4096,512]{1,0:T(8,128)} %all-gather.11.cloned.1.call-done), kind=kOutput, calls=%fused_computation.1 | convolution fusion | flops 25771376640 | bytes 29360128 | tf_op jit(solution)/shard_map/dot_general | solution.py:24
  462.1 0.0 all-gather.15.cloned.1.call-update
  462.1 0.0 all-gather.13.cloned.1.call-start
  462.1 0.5 all-gather.13.cloned.1.call-update
  462.7 0.0 copy-start.1
  462.7 0.3 all-gather.17.cloned.1.call-start
  463.0 57.6 %all-gather.15.cloned.1.call-done = f32[4096,512]{1,0:T(8,128)} async-done(((f32[1024,512]{1,0:T(8,128)}), f32[4096,512]{1,0:T(8,128)}) %all-gather.15.cloned.1.call-update) | async-done | bytes 8388624 | tf_op jit(solution)/shard_map/all_gather | solution.py:17
  520.5 229.3 %all-gather.13.cloned.1.call-done = f32[1024,4096]{1,0:T(8,128)} async-done(((f32[1024,512]{1,0:T(8,128)}), f32[1024,4096]{1,0:T(8,128)}) %all-gather.13.cloned.1.call-update) | async-done | bytes 16777232 | tf_op jit(solution)/shard_map/all_gather | solution.py:16
  749.8 31.0 %fusion.1 = f32[1024,512]{1,0:T(8,128)} fusion(f32[1024,4096]{1,0:T(8,128)} %all-gather.13.cloned.1.call-done, f32[4096,512]{1,0:T(8,128)} %all-gather.15.cloned.1.call-done), kind=kOutput, calls=%fused_computation.5 | convolution fusion | flops 25769803776 | bytes 27262976 | tf_op jit(solution)/shard_map/dot_general | solution.py:18
  780.9 0.0 all-gather.17.cloned.1.call-update
  780.9 56.6 %all-gather.17.cloned.1.call-done = f32[4096,512]{1,0:T(8,128)} async-done(((f32[1024,512]{1,0:T(8,128)}), f32[4096,512]{1,0:T(8,128)}) %all-gather.17.cloned.1.call-update) | async-done | bytes 8388624 | tf_op jit(solution)/shard_map/all_gather | solution.py:26
  837.5 0.0 copy-done.1
  837.5 31.2 %multiply_subtract_fusion = f32[1024,512]{1,0:T(8,128)} fusion(f32[1024,512]{1,0:T(8,128)S(1)} %copy-done.1, f32[1024,4096]{1,0:T(8,128)} %all-gather.13.cloned.1.call-done, f32[4096,512]{1,0:T(8,128)} %all-gather.17.cloned.1.call-done), kind=kOutput, calls=%fused_computation | convolution fusion | flops 25771376640 | bytes 29360128 | tf_op jit(solution)/shard_map/dot_general | solution.py:24
Async XLA Ops:
  6.5 107.2 %all-gather.9.cloned.1.call-start = ((), (), s32[]{:S(2)}) async-start(), calls=%async_computation.1 | async-start | bytes 10485760 | tf_op jit(solution)/shard_map/all_gather | solution.py:17
  55.3 287.9 %all-gather.7.cloned.1.call-start = ((), (), s32[]{:S(2)}) async-start(), calls=%async_computation | async-start | bytes 18874368 | tf_op jit(solution)/shard_map/all_gather | solution.py:16
  56.1 374.8 %copy-start = (f32[1024,512]{1,0:T(8,128)S(1)}, f32[1024,512]{1,0:T(8,128)}, u32[]{:S(2)}) copy-start(f32[1024,512]{1,0:T(8,128)} %broadcast_multiply_fusion) | copy-start | bytes 6291460
  56.1 374.8 %all-gather.11.cloned.1.call-start = ((), (), s32[]{:S(2)}) async-start(), calls=%async_computation.2 | async-start | bytes 10485760 | tf_op jit(solution)/shard_map/all_gather | solution.py:26
  374.2 146.3 %all-gather.15.cloned.1.call-start = ((), (), s32[]{:S(2)}) async-start(), calls=%async_computation.4 | async-start | bytes 10485760 | tf_op jit(solution)/shard_map/all_gather | solution.py:17
  462.1 287.7 %all-gather.13.cloned.1.call-start = ((), (), s32[]{:S(2)}) async-start(), calls=%async_computation.3 | async-start | bytes 18874368 | tf_op jit(solution)/shard_map/all_gather | solution.py:16
  462.7 374.8 %copy-start.1 = (f32[1024,512]{1,0:T(8,128)S(1)}, f32[1024,512]{1,0:T(8,128)}, u32[]{:S(2)}) copy-start(f32[1024,512]{1,0:T(8,128)} %multiply_subtract_fusion.1) | copy-start | bytes 6291460
  462.7 374.8 %all-gather.17.cloned.1.call-start = ((), (), s32[]{:S(2)}) async-start(), calls=%async_computation.5 | async-start | bytes 10485760 | tf_op jit(solution)/shard_map/all_gather | solution.py:26
Sparse Core Ops, SparseCore 0:
  55.4 58.2 all-gather.8
  115.9 227.2 all-gather.6
  374.4 56.4 all-gather.10
  462.2 58.2 all-gather.14
  522.6 227.2 all-gather.12
  781.0 56.4 all-gather.16
where the time goes:
time: 876 us
  waiting for transfers between devices  688 us (79%)
  matrix products  125 us (14%)
  blocking collectives  42.2 us (5%)
  between operations  14.2 us (2%)
    all_gather x2, waiting for transfers between devices, shards(): rows_panel = lax.all_gather(source, 'col', axis=1, tiled=True)  459 us
    all_gather x2, waiting for transfers between devices, shards(): cols_panel = lax.all_gather(source, 'row', axis=0, tiled=True)  115 us
    all_gather x2, waiting for transfers between devices, shards(): lax.all_gather(square, 'row', axis=0, tiled=True)  113 us
    dot_general x2, matrix products, shards(): jnp.dot(rows_panel, lax.all_gather(square, 'row', axis=0, tiled=True), pr...  62.5 us
    dot_general x2, matrix products, shards(): jnp.dot(rows_panel, cols_panel, preferred_element_type=jnp.float32, preci...  62 us
    psum x1, blocking collectives, shards(): total = lax.psum(jnp.sum(matrix * matrix), ('row', 'col'))  42.2 us
  transfers between devices with their start and end apart: 6, of which 6 were waited for; matrix products, arithmetic and copies ran while one was open for 0% of the time, Pallas kernels for 0%

commit v1 on v0

--- a/solution.py
+++ b/solution.py
@@ -14,7 +14,14 @@
     for step in range(ITERS):
         source = x_iter
         rows_panel = lax.all_gather(source, "col", axis=1, tiled=True)
-        cols_panel = lax.all_gather(source, "row", axis=0, tiled=True)
+        ring = [source]
+        for hop in range(3):
+            ring.append(lax.ppermute(ring[-1], "row", [(dev, (dev + 1) % 4) for dev in range(4)]))
+        cols_panel = jnp.roll(
+            jnp.concatenate(ring[::-1], axis=0),
+            (lax.axis_index("row") + 1) * ring[0].shape[0],
+            axis=0,
+        )
         square = jnp.dot(
             rows_panel,
             cols_panel,

time: 876 us -> 768 us (0.88)
  waiting for transfers between devices: 688 us -> 563 us
  matrix products: 125 us -> 138 us
    all_gather x2, waiting for transfers between devices: 459 us -> 297 us  [shards(): rows_panel = lax.all_gather(source, 'col', axis=1, tiled=True)]
    ppermute x0 -> x6, waiting for transfers between devices: none -> 153 us  [shards(): lax.ppermute(ring[-1], 'row', [(dev, (dev + 1) % 4) for dev in range(4)])]
    all_gather x2 -> x0, waiting for transfers between devices: 115 us -> none  [shards(): cols_panel = lax.all_gather(source, 'row', axis=0, tiled=True)]
    dot_general x2, matrix products: 62 us -> 75.5 us  [shards(): jnp.dot(rows_panel, cols_panel, preferred_element_type=jnp.float32, preci...]
  transfers between devices with their start and end apart: 6 -> 10, of which waited for: 6 -> 10; matrix products, arithmetic and copies ran while one was open for 0% -> 0% of each run, Pallas kernels for 0% -> 0%
where the time goes in v1:
time: 768 us
  waiting for transfers between devices  563 us (73%)
  matrix products  138 us (18%)
  blocking collectives  42.2 us (5%)
  between operations  13.9 us (2%)
    all_gather x2, waiting for transfers between devices, shards(): rows_panel = lax.all_gather(source, 'col', axis=1, tiled=True)  297 us
    ppermute x6, waiting for transfers between devices, shards(): lax.ppermute(ring[-1], 'row', [(dev, (dev + 1) % 4) for dev in range(4)])  153 us
    all_gather x2, waiting for transfers between devices, shards(): lax.all_gather(square, 'row', axis=0, tiled=True)  113 us
    dot_general x2, matrix products, shards(): jnp.dot(rows_panel, cols_panel, preferred_element_type=jnp.float32, preci...  75.5 us
    dot_general x2, matrix products, shards(): jnp.dot(rows_panel, lax.all_gather(square, 'row', axis=0, tiled=True), pr...  62.5 us
    psum x1, blocking collectives, shards(): total = lax.psum(jnp.sum(matrix * matrix), ('row', 'col'))  42.2 us
  transfers between devices with their start and end apart: 10, of which 10 were waited for; matrix products, arithmetic and copies ran while one was open for 0% of the time, Pallas kernels for 0%

profile of v1, /device:TPU:0, one launch (start us, length us, event | category | flops | bytes accessed | tf_op | source)
XLA Modules:
  0.0 768.0 jit_solution(5348244995914458045)
XLA Ops:
  6.5 0.0 all-gather.5.cloned.1.call-start
  6.5 2.7 multiply_reduce_fusion
  9.3 42.2 %psum.7 = f32[]{:T(128)} all-reduce(f32[]{:T(128)} %multiply_reduce_fusion), channel_id=1, replica_groups=mesh['row'=4,'col'=8] {'row','col'}, use_global_device_ids=true, to_apply=%region_1.0 | all-reduce | flops 1 | bytes 8 | tf_op jit(solution)/shard_map/psum | solution.py:11
  52.2 3.1 broadcast_multiply_fusion
  55.3 0.0 all-gather.5.cloned.1.call-update
  55.3 0.0 all-gather.7.cloned.1.call-start
  55.4 0.1 collective-permute-start
  55.4 25.7 %collective-permute-done = f32[1024,512]{1,0:T(8,128)S(1)} collective-permute-done((f32[1024,512]{1,0:T(8,128)}, f32[1024,512]{1,0:T(8,128)S(1)}, u32[]{:S(2)}, u32[]{:S(2)}) %collective-permute-start) | collective-permute-done | bytes 2097184 | tf_op jit(solution)/shard_map/ppermute | solution.py:19
  81.1 0.0 copy-start.2
  81.1 1.3 copy-done.2
  82.4 0.2 collective-permute-start.1
  82.7 25.4 %collective-permute-done.1 = f32[1024,512]{1,0:T(8,128)} collective-permute-done((f32[1024,512]{1,0:T(8,128)S(1)}, f32[1024,512]{1,0:T(8,128)}, u32[]{:S(2)}, u32[]{:S(2)}) %collective-permute-start.1) | collective-permute-done | bytes 2097184 | tf_op jit(solution)/shard_map/ppermute | solution.py:19
  108.0 0.0 collective-permute-start.2
  108.0 0.0 copy-start
  108.0 25.8 %collective-permute-done.2 = f32[1024,512]{1,0:T(8,128)} collective-permute-done((f32[1024,512]{1,0:T(8,128)}, f32[1024,512]{1,0:T(8,128)}, u32[]{:S(2)}, u32[]{:S(2)}) %collective-permute-start.2) | collective-permute-done | bytes 2097184 | tf_op jit(solution)/shard_map/ppermute | solution.py:19
  133.8 148.9 %all-gather.5.cloned.1.call-done = f32[1024,4096]{1,0:T(8,128)} async-done(((f32[1024,512]{1,0:T(8,128)}), f32[1024,4096]{1,0:T(8,128)}) %all-gather.5.cloned.1.call-update) | async-done | bytes 16777232 | tf_op jit(solution)/shard_map/all_gather | solution.py:16
  282.7 37.8 %fusion.14 = f32[1024,512]{1,0:T(8,128)} fusion(f32[1024,4096]{1,0:T(8,128)} %all-gather.5.cloned.1.call-done, s32[]{:T(128)S(6)} %select_n.13, f32[1024,512]{1,0:T(8,128)} %collective-permute-done.2, f32[1024,512]{1,0:T(8,128)} %collective-permute-done.1, f32[1024,512]{1,0:T(8,128)} %copy-done.2, f32[1024,512]{1,0:T(8,128)} %broadcast_multiply_fusion), kind=kOutput, calls=%fused_computation.28 | convolution fusion | flops 25784483840 | bytes 27262980 | tf_op jit(solution)/shard_map/dot_general | solution.py:25
  320.5 0.0 all-gather.7.cloned.1.call-update
  320.5 0.2 all-gather.9.cloned.1.call-start
  320.7 56.4 %all-gather.7.cloned.1.call-done = f32[4096,512]{1,0:T(8,128)} async-done(((f32[1024,512]{1,0:T(8,128)}), f32[4096,512]{1,0:T(8,128)}) %all-gather.7.cloned.1.call-update) | async-done | bytes 8388624 | tf_op jit(solution)/shard_map/all_gather | solution.py:33
  377.1 0.0 copy-done
  377.1 31.2 %multiply_subtract_fusion.1 = f32[1024,512]{1,0:T(8,128)} fusion(f32[1024,512]{1,0:T(8,128)S(1)} %copy-done, f32[1024,4096]{1,0:T(8,128)} %all-gather.5.cloned.1.call-done, f32[4096,512]{1,0:T(8,128)} %all-gather.7.cloned.1.call-done), kind=kOutput, calls=%fused_computation.33 | convolution fusion | flops 25771376640 | bytes 29360128 | tf_op jit(solution)/shard_map/dot_general | solution.py:31
  408.4 0.0 all-gather.9.cloned.1.call-update
  408.4 0.0 copy-start.1
  408.4 0.0 all-gather.11.cloned.1.call-start
  408.4 0.3 collective-permute-start.3
  408.7 25.4 %collective-permute-done.3 = f32[1024,512]{1,0:T(8,128)S(1)} collective-permute-done((f32[1024,512]{1,0:T(8,128)}, f32[1024,512]{1,0:T(8,128)S(1)}, u32[]{:S(2)}, u32[]{:S(2)}) %collective-permute-start.3) | collective-permute-done | bytes 2097184 | tf_op jit(solution)/shard_map/ppermute | solution.py:19
  434.2 0.0 copy-start.3
  434.2 1.3 copy-done.3
  435.5 0.0 collective-permute-start.4
  435.5 25.5 %collective-permute-done.4 = f32[1024,512]{1,0:T(8,128)S(1)} collective-permute-done((f32[1024,512]{1,0:T(8,128)S(1)}, f32[1024,512]{1,0:T(8,128)S(1)}, u32[]{:S(2)}, u32[]{:S(2)}) %collective-permute-start.4) | collective-permute-done | bytes 2097184 | tf_op jit(solution)/shard_map/ppermute | solution.py:19
  461.0 0.0 copy-start.4
  461.0 1.3 copy-done.4
  462.3 0.0 collective-permute-start.5
  462.3 25.6 %collective-permute-done.5 = f32[1024,512]{1,0:T(8,128)} collective-permute-done((f32[1024,512]{1,0:T(8,128)S(1)}, f32[1024,512]{1,0:T(8,128)}, u32[]{:S(2)}, u32[]{:S(2)}) %collective-permute-start.5) | collective-permute-done | bytes 2097184 | tf_op jit(solution)/shard_map/ppermute | solution.py:19
  487.9 147.9 %all-gather.9.cloned.1.call-done = f32[1024,4096]{1,0:T(8,128)} async-done(((f32[1024,512]{1,0:T(8,128)}), f32[1024,4096]{1,0:T(8,128)}) %all-gather.9.cloned.1.call-update) | async-done | bytes 16777232 | tf_op jit(solution)/shard_map/all_gather | solution.py:16
  635.8 37.8 %fusion.4 = f32[1024,512]{1,0:T(8,128)} fusion(f32[1024,4096]{1,0:T(8,128)} %all-gather.9.cloned.1.call-done, s32[]{:T(128)S(6)} %select_n.13, f32[1024,512]{1,0:T(8,128)} %collective-permute-done.5, f32[1024,512]{1,0:T(8,128)} %copy-done.4, f32[1024,512]{1,0:T(8,128)} %copy-done.3, f32[1024,512]{1,0:T(8,128)} %multiply_subtract_fusion.1), kind=kOutput, calls=%fused_computation.20 | convolution fusion | flops 25784483840 | bytes 27262980 | tf_op jit(solution)/shard_map/dot_general | solution.py:25
  673.5 0.0 all-gather.11.cloned.1.call-update
  673.6 56.6 %all-gather.11.cloned.1.call-done = f32[4096,512]{1,0:T(8,128)} async-done(((f32[1024,512]{1,0:T(8,128)}), f32[4096,512]{1,0:T(8,128)}) %all-gather.11.cloned.1.call-update) | async-done | bytes 8388624 | tf_op jit(solution)/shard_map/all_gather | solution.py:33
  730.2 0.0 copy-done.1
  730.2 31.2 %multiply_subtract_fusion = f32[1024,512]{1,0:T(8,128)} fusion(f32[1024,512]{1,0:T(8,128)S(1)} %copy-done.1, f32[1024,4096]{1,0:T(8,128)} %all-gather.9.cloned.1.call-done, f32[4096,512]{1,0:T(8,128)} %all-gather.11.cloned.1.call-done), kind=kOutput, calls=%fused_computation.32 | convolution fusion | flops 25771376640 | bytes 29360128 | tf_op jit(solution)/shard_map/dot_general | solution.py:31
Async XLA Ops:
  6.5 276.2 %all-gather.5.cloned.1.call-start = ((), (), s32[]{:S(2)}) async-start(), calls=%async_computation | async-start | bytes 18874368 | tf_op jit(solution)/shard_map/all_gather | solution.py:16
  55.3 321.8 %all-gather.7.cloned.1.call-start = ((), (), s32[]{:S(2)}) async-start(), calls=%async_computation.1 | async-start | bytes 10485760 | tf_op jit(solution)/shard_map/all_gather | solution.py:33
  55.4 25.7 %collective-permute-start = (f32[1024,512]{1,0:T(8,128)}, f32[1024,512]{1,0:T(8,128)S(1)}, u32[]{:S(2)}, u32[]{:S(2)}) collective-permute-start(f32[1024,512]{1,0:T(8,128)} %broadcast_multiply_fusion), channel_id=1, source_target_pairs={{0,8},{8,16},{16,24},{24,0},{1,9},{9,17},{17,25},{25,1},{2,10},{10... | collective-permute-start | bytes 6291464 | tf_op jit(solution)/shard_map/ppermute | solution.py:19
  81.1 1.3 copy-start.2
  82.4 25.6 %collective-permute-start.1 = (f32[1024,512]{1,0:T(8,128)S(1)}, f32[1024,512]{1,0:T(8,128)}, u32[]{:S(2)}, u32[]{:S(2)}) collective-permute-start(f32[1024,512]{1,0:T(8,128)S(1)} %collective-permute-done), channel_id=1, source_target_pairs={{0,8},{8,16},{16,24},{24,0},{1,9},{9,17},{17,25},{25,1},{2,10},{10... | collective-permute-start | bytes 6291464 | tf_op jit(solution)/shard_map/ppermute | solution.py:19
  108.0 25.8 %collective-permute-start.2 = (f32[1024,512]{1,0:T(8,128)}, f32[1024,512]{1,0:T(8,128)}, u32[]{:S(2)}, u32[]{:S(2)}) collective-permute-start(f32[1024,512]{1,0:T(8,128)} %collective-permute-done.1), channel_id=1, source_target_pairs={{0,8},{8,16},{16,24},{24,0},{1,9},{9,17},{17,25},{25,1},{2,10},{10... | collective-permute-start | bytes 6291464 | tf_op jit(solution)/shard_map/ppermute | solution.py:19
  108.0 269.1 %copy-start = (f32[1024,512]{1,0:T(8,128)S(1)}, f32[1024,512]{1,0:T(8,128)}, u32[]{:S(2)}) copy-start(f32[1024,512]{1,0:T(8,128)} %broadcast_multiply_fusion) | copy-start | bytes 6291460
  320.5 315.3 %all-gather.9.cloned.1.call-start = ((), (), s32[]{:S(2)}) async-start(), calls=%async_computation.2 | async-start | bytes 18874368 | tf_op jit(solution)/shard_map/all_gather | solution.py:16
  408.4 321.8 %copy-start.1 = (f32[1024,512]{1,0:T(8,128)S(1)}, f32[1024,512]{1,0:T(8,128)}, u32[]{:S(2)}) copy-start(f32[1024,512]{1,0:T(8,128)} %multiply_subtract_fusion.1) | copy-start | bytes 6291460
  408.4 321.8 %all-gather.11.cloned.1.call-start = ((), (), s32[]{:S(2)}) async-start(), calls=%async_computation.3 | async-start | bytes 10485760 | tf_op jit(solution)/shard_map/all_gather | solution.py:33
  408.4 25.7 %collective-permute-start.3 = (f32[1024,512]{1,0:T(8,128)}, f32[1024,512]{1,0:T(8,128)S(1)}, u32[]{:S(2)}, u32[]{:S(2)}) collective-permute-start(f32[1024,512]{1,0:T(8,128)} %multiply_subtract_fusion.1), channel_id=1, source_target_pairs={{0,8},{8,16},{16,24},{24,0},{1,9},{9,17},{17,25},{25,1},{2,10},{10... | collective-permute-start | bytes 6291464 | tf_op jit(solution)/shard_map/ppermute | solution.py:19
  434.2 1.3 copy-start.3
  435.5 25.5 %collective-permute-start.4 = (f32[1024,512]{1,0:T(8,128)S(1)}, f32[1024,512]{1,0:T(8,128)S(1)}, u32[]{:S(2)}, u32[]{:S(2)}) collective-permute-start(f32[1024,512]{1,0:T(8,128)S(1)} %collective-permute-done.3), channel_id=1, source_target_pairs={{0,8},{8,16},{16,24},{24,0},{1,9},{9,17},{17,25},{25,1},{2,10},{10... | collective-permute-start | bytes 6291464 | tf_op jit(solution)/shard_map/ppermute | solution.py:19
  461.0 1.3 copy-start.4
  462.3 25.6 %collective-permute-start.5 = (f32[1024,512]{1,0:T(8,128)S(1)}, f32[1024,512]{1,0:T(8,128)}, u32[]{:S(2)}, u32[]{:S(2)}) collective-permute-start(f32[1024,512]{1,0:T(8,128)S(1)} %collective-permute-done.4), channel_id=1, source_target_pairs={{0,8},{8,16},{16,24},{24,0},{1,9},{9,17},{17,25},{25,1},{2,10},{10... | collective-permute-start | bytes 6291464 | tf_op jit(solution)/shard_map/ppermute | solution.py:19
Sparse Core Ops, SparseCore 0:
  55.4 227.2 all-gather.4
  320.6 56.4 all-gather.6
  408.5 227.2 all-gather.8
  673.7 56.4 all-gather.10
